TPU v7x, 32 devices: a whole 2x2x4 slice. The times are simulated.
32 devices in a mesh: ctx: 8 (over z, x), rep: 4 (over y, core).
Axes of the slice: x: 2, y: 2, z: 4, core: 2. Of those that a mesh axis runs over, the one named last changes fastest.
Arguments:
- latents: bfloat16 [131072, 576], P(('ctx', 'rep')), may hold values from -6 to 6
- queries: bfloat16 [64, 73728], P('rep', 'ctx'), may hold values from -4000 to 4000, as said below
- hot_ids: int32 [16], P('ctx'), may hold values from 0 to 15, as said below
- lengths: int32 [64], P('rep'), may hold values from 65536 to 131072
Outputs:
- attended: bfloat16 [64, 65536], P('rep', 'ctx')
Inputs may be any that keep to these rules, and one draw needn't show every extreme that they name: `queries`: query entries lie in the stated range. `hot_ids`: entries g * 2 to (g + 1) * 2 - 1 are distinct block numbers within group g.
All inputs are finite; a program needn't handle non-finite values.
Results may differ from a plain program's by a relative error of at most 0.0031.
Values may be sent and summed in bfloat16 or wider, within the bound.
A program may use at most 128 MiB of HBM per device.

v0:
```python
import jax
import jax.numpy as jnp
from jax import lax
from jax.sharding import PartitionSpec as P

H = 128
LAT = 512
ROPE = 64
QK = 192
BLK = 1024
HOT_GRP = 2


def from_root(block, axis, holder):
    block = jnp.where(lax.axis_index(axis) == holder, block, jnp.zeros_like(block))
    return lax.psum(block, axis)


def on_device(latents, queries, hot_ids, lengths):
    row_width = LAT + ROPE
    score_scale = QK ** (-0.5)
    rep_count = lax.axis_size("rep")
    group_index = lax.axis_index("ctx")
    per_device = latents.shape[0] // BLK
    blocks_held = []
    for slot_index in range(HOT_GRP):
        owner_index = hot_ids[slot_index] // per_device
        local_block = lax.dynamic_slice_in_dim(
            latents, hot_ids[slot_index] % per_device * BLK, BLK, 0
        )
        blocks_held.append(from_root(local_block, "rep", owner_index))
    key_rows = jnp.concatenate(blocks_held, axis=0)
    value_rows = key_rows[:, :LAT]
    offsets = jnp.arange(BLK, dtype=jnp.int32)
    row_index = (
        (group_index * (rep_count * per_device) + hot_ids)[:, None] * BLK + offsets[None, :]
    ).reshape(-1)
    all_heads = lax.all_gather(queries, "ctx", axis=1, tiled=True)
    query_count = all_heads.shape[0]
    query_blocks = all_heads.reshape(query_count // 4, 4, H, row_width)
    span_blocks = lengths.reshape(query_count // 4, 4)

    def partial_value(item_pair):
        query_block, span_block = item_pair
        scores = (
            jnp.einsum("qhw,kw->qhk", query_block, key_rows, preferred_element_type=jnp.float32)
            * score_scale
        )
        visible = row_index[None, None, :] < span_block[:, None, None]
        peak_score = jnp.max(jnp.where(visible, scores, -1e30), axis=2)
        exponent = jnp.where(visible, scores - peak_score[:, :, None], -1e30)
        weights = jnp.exp(exponent).astype(jnp.bfloat16)
        totals = jnp.sum(weights, axis=2, dtype=jnp.float32)
        numerators = jnp.einsum(
            "qhk,kl->qhl", weights, value_rows, preferred_element_type=jnp.float32
        )
        return (numerators, peak_score, totals)

    numerators, peak_score, totals = lax.map(partial_value, (query_blocks, span_blocks))
    numerators = numerators.reshape(query_count, H, LAT)
    peak_score = peak_score.reshape(query_count, H)
    totals = totals.reshape(query_count, H)
    all_numer, all_peak, all_total = (
        lax.all_to_all(numerators[None], "ctx", split_axis=2, concat_axis=0, tiled=True),
        lax.all_to_all(peak_score[None], "ctx", split_axis=2, concat_axis=0, tiled=True),
        lax.all_to_all(totals[None], "ctx", split_axis=2, concat_axis=0, tiled=True),
    )
    overall = jnp.max(all_peak, axis=0)
    factor = jnp.exp(all_peak - overall[None])
    merged = jnp.sum(all_numer * factor[..., None], axis=0)
    weight_sum = jnp.sum(all_total * factor, axis=0)
    return (merged / weight_sum[..., None]).reshape(query_count, -1).astype(jnp.bfloat16)


def solution(mesh):
    placed = (P(("ctx", "rep"), None), P("rep", "ctx"), P("ctx"), P("rep"))
    return jax.shard_map(
        on_device, mesh=mesh, in_specs=placed, out_specs=P("rep", "ctx"), check_vma=False
    )
```

profile of v0, /device:TPU:0, one launch (start us, length us, event | category | flops | bytes accessed | tf_op | source)
XLA Modules:
  0.0 254.2 jit_solution(5459596877738601110)
XLA Ops:
  7.4 0.0 all-reduce.3.cloned.1.call-start
  7.4 1.4 fusion.19
  13.9 3.7 %dynamic-slice_select_fusion = (bf16[1024,576]{0,1:T(8,128)(2,1)}, bf16[1024,576]{0,1:T(8,128)(2,1)}) fusion(bf16[4096,576]{0,1:T(8,128)(2,1)} %param.6, s32[]{:T(128)S(6)} %select_n.53, pred[]{:T(512)S(6)} %eq.10, s32[]{:T(128)S(6)} %select_n.48, pred[]{:T(512)S(6)} %eq.9), kind=kLoop, calls=%fused_computation.23 | loop fusion | flops 1179648 | bytes 4718602 | tf_op jit(solution)/shard_map/jit(_where)/select_n | solution.py:15
  17.6 0.0 all-reduce.3.cloned.1.call-update
  17.6 0.0 all-gather.2.cloned.1.call-start
  17.6 0.5 all-gather.2.cloned.1.call-update
  18.2 0.0 copy-done.2
  18.2 0.1 reshape.57
  18.3 0.0 copy-done.1
  18.3 57.9 %all-reduce.3.cloned.1.call-done = (bf16[1024,576]{0,1:T(8,128)(2,1)}, bf16[1024,576]{0,1:T(8,128)(2,1)}) async-done(((bf16[1024,576]{0,1:T(8,128)(2,1)}, bf16[1024,576]{0,1:T(8,128)(2,1)}), (bf16[1024,576]{0,1:T(8,128)(2,1)}, bf16[1024,576]{0,1:T(8,128)(2,1)})) %all-reduce.3.cloned.1.call-update) | async-done | bytes 2359312 | tf_op jit(solution)/shard_map/psum | solution.py:16
  76.1 1.4 constant_dynamic-update-slice_fusion.1
  77.5 1.4 constant_dynamic-update-slice_fusion
  78.9 1.5 slice.14
  80.4 3.9 %copy.30 = bf16[2048,512]{1,0:T(8,128)(2,1)} copy(bf16[2048,512]{0,1:T(8,128)(2,1)} %slice.14) | data formatting | bytes 4194304
  84.3 5.5 %reshape.58 = bf16[4,4,128,576]{3,2,1,0:T(8,128)(2,1)} reshape(bf16[16,73728]{1,0:T(8,128)(2,1)} %all-gather.2.cloned.1.call-done) | data formatting | bytes 4718592 | tf_op jit(solution)/shard_map/reshape | solution.py:40
  89.8 4.4 %copy.24 = bf16[4,4,128,576]{2,3,1,0:T(8,128)(2,1)} copy(bf16[4,4,128,576]{3,2,1,0:T(8,128)(2,1)} %reshape.58) | data formatting | bytes 4718592
  94.2 27.9 %while.15 = (s32[]{:T(128)}, f32[4,4,128,512]{3,2,1,0:T(8,128)}, f32[4,4,128]{2,1,0:T(4,128)S(1)}, f32[4,4,128]{2,1,0:T(4,128)S(1)}, s32[4,4]{1,0:T(4,128)S(1)},...) while((s32[]{:T(128)}, f32[4,4,128,512]{3,2,1,0:T(8,128)}, ...), condition=%wide.region_5.6_spmd.clone, body=%wide.region_2.5_spmd.clone.sunk | while | flops 2295342080 | bytes 27149504 | solution.py:59
  94.2 0.1 add_bitcast_fusion.2
  94.3 0.1 broadcast_compare_fusion.2
  94.4 0.0 copy-start
  94.4 3.4 %select_reduce_fusion.2 = (f32[4,128]{1,0:T(4,128)S(1)}, f32[4,128,2048]{2,1,0:T(8,128)S(1)}) fusion(pred[4,2048]{1,0:T(4,128)(4,1)S(1)} %broadcast_compare_fusion.2, bf16[2048,576]{0,1:T(8,128)(2,1)S(1)} %get-tuple-element.242, bf16[4,4,128,576]{2,3,1,0:T(8,128)(2,1)} %get-tuple-element.241, s32[]{:T(128)} %get-tuple-element.226), kind=kOutput, calls=%fused_computation.3.clone.1 | convolution fusion | flops 1211104768 | bytes 7154176 | tf_op jit(solution)/shard_map/while/body/eval_jaxpr/qhw,kw->qhk/dot_general | solution.py:46
  97.7 1.1 convert_reduce_fusion.2
  98.8 0.0 copy-done
  98.8 2.3 fusion.25
  101.2 0.1 add_bitcast_fusion.2
  101.2 0.1 broadcast_compare_fusion.2
  101.3 0.0 copy-start
  101.3 3.4 %select_reduce_fusion.2 = (f32[4,128]{1,0:T(4,128)S(1)}, f32[4,128,2048]{2,1,0:T(8,128)S(1)}) fusion(pred[4,2048]{1,0:T(4,128)(4,1)S(1)} %broadcast_compare_fusion.2, bf16[2048,576]{0,1:T(8,128)(2,1)S(1)} %get-tuple-element.242, bf16[4,4,128,576]{2,3,1,0:T(8,128)(2,1)} %get-tuple-element.241, s32[]{:T(128)} %get-tuple-element.226), kind=kOutput, calls=%fused_computation.3.clone.1 | convolution fusion | flops 1211104768 | bytes 7154176 | tf_op jit(solution)/shard_map/while/body/eval_jaxpr/qhw,kw->qhk/dot_general | solution.py:46
  104.7 1.1 convert_reduce_fusion.2
  105.8 0.0 copy-done
  105.8 2.4 fusion.25
  108.2 0.1 add_bitcast_fusion.2
  108.2 0.1 broadcast_compare_fusion.2
  108.3 0.0 copy-start
  108.3 3.4 %select_reduce_fusion.2 = (f32[4,128]{1,0:T(4,128)S(1)}, f32[4,128,2048]{2,1,0:T(8,128)S(1)}) fusion(pred[4,2048]{1,0:T(4,128)(4,1)S(1)} %broadcast_compare_fusion.2, bf16[2048,576]{0,1:T(8,128)(2,1)S(1)} %get-tuple-element.242, bf16[4,4,128,576]{2,3,1,0:T(8,128)(2,1)} %get-tuple-element.241, s32[]{:T(128)} %get-tuple-element.226), kind=kOutput, calls=%fused_computation.3.clone.1 | convolution fusion | flops 1211104768 | bytes 7154176 | tf_op jit(solution)/shard_map/while/body/eval_jaxpr/qhw,kw->qhk/dot_general | solution.py:46
  111.7 1.1 convert_reduce_fusion.2
  112.8 2.3 fusion.25
  115.1 0.1 add_bitcast_fusion.2
  115.2 0.1 broadcast_compare_fusion.2
  115.3 0.0 copy-start
  115.3 3.4 %select_reduce_fusion.2 = (f32[4,128]{1,0:T(4,128)S(1)}, f32[4,128,2048]{2,1,0:T(8,128)S(1)}) fusion(pred[4,2048]{1,0:T(4,128)(4,1)S(1)} %broadcast_compare_fusion.2, bf16[2048,576]{0,1:T(8,128)(2,1)S(1)} %get-tuple-element.242, bf16[4,4,128,576]{2,3,1,0:T(8,128)(2,1)} %get-tuple-element.241, s32[]{:T(128)} %get-tuple-element.226), kind=kOutput, calls=%fused_computation.3.clone.1 | convolution fusion | flops 1211104768 | bytes 7154176 | tf_op jit(solution)/shard_map/while/body/eval_jaxpr/qhw,kw->qhk/dot_general | solution.py:46
  118.6 1.1 convert_reduce_fusion.2
  119.8 2.3 fusion.25
  122.1 0.1 copy.26
  122.2 0.5 broadcast.54
  122.7 0.7 reduce.3
  123.4 0.7 reshape.61
  124.1 5.5 %all-to-all-start.1 = ((f32[8,1,256]{2,1,0:T(1,128)}), f32[8,1,256]{2,1,0:T(1,128)S(1)}, u32[]{:S(2)}, u32[]{:S(2)}) async-start(f32[8,1,256]{2,1,0:T(1,128)} %reshape.61), calls=%async_computation.1 | async-start | bytes 16384 | tf_op jit(solution)/shard_map/all_to_all | solution.py:65
  129.6 0.1 copy.27
  129.7 0.7 reduce.1
  130.4 0.7 reshape.63
  131.1 5.0 %all-to-all-done.1 = f32[8,1,256]{2,1,0:T(1,128)S(1)} async-done(((f32[8,1,256]{2,1,0:T(1,128)}), f32[8,1,256]{2,1,0:T(1,128)S(1)}, u32[]{:S(2)}, u32[]{:S(2)}) %all-to-all-start.1) | async-done | bytes 8224 | tf_op jit(solution)/shard_map/all_to_all | solution.py:65
  136.1 3.3 %all-to-all-start.2 = ((f32[8,1,256]{2,1,0:T(1,128)}), f32[8,1,256]{2,1,0:T(1,128)S(1)}, u32[]{:S(2)}, u32[]{:S(2)}) async-start(f32[8,1,256]{2,1,0:T(1,128)} %reshape.63), calls=%async_computation.2 | async-start | bytes 16384 | tf_op jit(solution)/shard_map/all_to_all | solution.py:66
  139.5 6.6 %copy.29 = f32[1,16,128,512]{3,1,0,2:T(8,128)} copy(f32[1,16,128,512]{3,2,1,0:T(8,128)} %bitcast.2) | data formatting | bytes 8388608 | tf_op jit(solution)/shard_map/broadcast_in_dim;reshape | solution.py:64
  146.0 0.0 all-to-all-done.2
  146.1 5.9 %all-to-all-start = ((f32[1,16,128,512]{3,1,0,2:T(8,128)}), f32[1,16,128,512]{3,1,0,2:T(8,128)}, u32[]{:S(2)}, u32[]{:S(2)}) async-start(f32[1,16,128,512]{3,1,0,2:T(8,128)} %copy.29), calls=%async_computation | async-start | bytes 8388608 | tf_op jit(solution)/shard_map/all_to_all | solution.py:64
  152.0 0.6 reduce.4
  152.6 0.1 reshape.62
  152.7 0.6 reduce.2
  153.3 0.1 reshape.64
  153.5 89.8 %all-to-all-done = f32[1,16,128,512]{3,1,0,2:T(8,128)} async-done(((f32[1,16,128,512]{3,1,0,2:T(8,128)}), f32[1,16,128,512]{3,1,0,2:T(8,128)}, u32[]{:S(2)}, u32[]{:S(2)}) %all-to-all-start) | async-done | bytes 4194336 | tf_op jit(solution)/shard_map/all_to_all | solution.py:64
  243.3 2.6 %multiply_reduce_fusion = f32[16,16,512]{2,0,1:T(8,128)S(1)} fusion(f32[8,16,16,512]{3,1,2,0:T(8,128)} %bitcast.5, f32[8,16,16]{1,2,0:T(8,128)S(1)} %get-tuple-element.144), kind=kLoop, calls=%fused_computation.22 | loop fusion | flops 1966080 | bytes 4726784 | tf_op jit(solution)/shard_map/reduce_sum | solution.py:70
  245.9 0.1 fusion.18
  246.0 0.7 copy.32
  (23 shorter events, 0.2 us)
Async XLA Ops:
  7.4 10.9 %copy-start.1 = (s32[2]{0:T(128)S(1)}, s32[2]{0:T(128)}, u32[]{:S(2)}) copy-start(s32[2]{0:T(128)} %param.8) | copy-start | bytes 28
  7.4 10.8 %copy-start.2 = (s32[16]{0:T(128)S(1)}, s32[16]{0:T(128)}, u32[]{:S(2)}) copy-start(s32[16]{0:T(128)} %param.9) | copy-start | bytes 196
  7.4 68.8 %all-reduce.3.cloned.1.call-start = ((), (), s32[]{:S(2)}) async-start(), calls=%async_computation.4 | async-start | bytes 4718592 | tf_op jit(solution)/shard_map/psum | solution.py:16
  17.6 66.7 %all-gather.2.cloned.1.call-start = ((), (), s32[]{:S(2)}) async-start(), calls=%async_computation.3 | async-start | bytes 2654208 | tf_op jit(solution)/shard_map/all_gather | solution.py:38
  94.4 4.5 %copy-start = (bf16[2048,512]{1,0:T(8,128)(2,1)S(1)}, bf16[2048,512]{1,0:T(8,128)(2,1)}, u32[]{:S(2)}) copy-start(bf16[2048,512]{1,0:T(8,128)(2,1)} %get-tuple-element.243) | copy-start | bytes 6291460 | tf_op jit(solution)/shard_map/while
  101.3 4.5 %copy-start = (bf16[2048,512]{1,0:T(8,128)(2,1)S(1)}, bf16[2048,512]{1,0:T(8,128)(2,1)}, u32[]{:S(2)}) copy-start(bf16[2048,512]{1,0:T(8,128)(2,1)} %get-tuple-element.243) | copy-start | bytes 6291460 | tf_op jit(solution)/shard_map/while
  108.3 4.5 %copy-start = (bf16[2048,512]{1,0:T(8,128)(2,1)S(1)}, bf16[2048,512]{1,0:T(8,128)(2,1)}, u32[]{:S(2)}) copy-start(bf16[2048,512]{1,0:T(8,128)(2,1)} %get-tuple-element.243) | copy-start | bytes 6291460 | tf_op jit(solution)/shard_map/while
  115.3 4.5 %copy-start = (bf16[2048,512]{1,0:T(8,128)(2,1)S(1)}, bf16[2048,512]{1,0:T(8,128)(2,1)}, u32[]{:S(2)}) copy-start(bf16[2048,512]{1,0:T(8,128)(2,1)} %get-tuple-element.243) | copy-start | bytes 6291460 | tf_op jit(solution)/shard_map/while
  124.1 12.0 %all-to-all-start.1 = ((f32[8,1,256]{2,1,0:T(1,128)}), f32[8,1,256]{2,1,0:T(1,128)S(1)}, u32[]{:S(2)}, u32[]{:S(2)}) async-start(f32[8,1,256]{2,1,0:T(1,128)} %reshape.61), calls=%async_computation.1 | async-start | bytes 16384 | tf_op jit(solution)/shard_map/all_to_all | solution.py:65
  136.1 9.9 %all-to-all-start.2 = ((f32[8,1,256]{2,1,0:T(1,128)}), f32[8,1,256]{2,1,0:T(1,128)S(1)}, u32[]{:S(2)}, u32[]{:S(2)}) async-start(f32[8,1,256]{2,1,0:T(1,128)} %reshape.63), calls=%async_computation.2 | async-start | bytes 16384 | tf_op jit(solution)/shard_map/all_to_all | solution.py:66
  146.1 97.3 %all-to-all-start = ((f32[1,16,128,512]{3,1,0,2:T(8,128)}), f32[1,16,128,512]{3,1,0,2:T(8,128)}, u32[]{:S(2)}, u32[]{:S(2)}) async-start(f32[1,16,128,512]{3,1,0,2:T(8,128)} %copy.29), calls=%async_computation | async-start | bytes 8388608 | tf_op jit(solution)/shard_map/all_to_all | solution.py:64
Sparse Core Ops, SparseCore 0:
  17.7 58.3 all-reduce.2
Sparse Core Ops, SparseCore 1:
  20.3 54.4 all-gather.1
where the time goes:
time: 255 us; the launch traced here: 254 us
  waiting for transfers between devices  153 us (60%)
  local copies, waits for them, and re-layouts  29.3 us (11%)
  matrix products  22.7 us (9%)
  between operations  20 us (8%)
  starting transfers between devices  14.8 us (6%)
  other arithmetic  14 us (5%)
    all_to_all x1, waiting for transfers between devices, on_device(): lax.all_to_all(numerators[None], 'ctx', split_axis=2, concat_axis=0, tile...  89.8 us
    psum x1, waiting for transfers between devices, from_root(): return lax.psum(block, axis)  57.9 us
    dot_general x4, matrix products, partial_value(): jnp.einsum('qhw,kw->qhk', query_block, key_rows, preferred_element_type=j...  13.4 us
    unnamed x12, local copies, waits for them, and re-layouts  11.9 us
    dot_general x4, matrix products, partial_value(): jnp.einsum('qhk,kl->qhl', weights, value_rows, preferred_element_type=jnp...  9.3 us
    another operation x1, local copies, waits for them, and re-layouts, on_device(): numerators[None]  6.59 us
    all_to_all x1, starting transfers between devices, on_device(): lax.all_to_all(numerators[None], 'ctx', split_axis=2, concat_axis=0, tile...  5.93 us
    all_to_all x1, starting transfers between devices, on_device(): lax.all_to_all(peak_score[None], 'ctx', split_axis=2, concat_axis=0, tile...  5.51 us
  transfers between devices with their start and end apart: 5, of which 3 were waited for; matrix products, arithmetic and copies ran while one was open for 7% of the time, Pallas kernels for 0%

commit v1 on v0

v1 whole, which is shorter than its diff:
```python
import functools

import jax
import jax.numpy as jnp
from jax import lax
from jax.experimental import pallas as pl
from jax.experimental.pallas import tpu as pltpu
from jax.sharding import PartitionSpec as P

H = 128
LAT = 512
ROPE = 64
QK = 192
BLK = 1024
HOT_GRP = 2
LANES = 128
PIECES = 8
SPAN = 512
MESH = pl.DeviceIdType.MESH


def kernel(
    n_ctx, n_rep, cand_ref, own_q_ref, base_ref, limit_ref, out_ref,
    from_core, merged, from_far, keys, heads, base_near, stat_send, stat_recv,
    part_send, part_recv, part_own, acc, peak_ref, total_ref, send_sem, recv_sem,
):
    outer = n_ctx // 2
    rows = own_q_ref.shape[0]
    piece = BLK // PIECES
    group = lax.axis_index("ctx")
    rep = lax.axis_index("rep")
    side = lax.rem(rep, 2)
    core = {"rep": rep + 1 - 2 * side}
    far = {"rep": lax.rem(rep + n_rep // 2, n_rep)}
    near = {"ctx": group + 1 - 2 * lax.rem(group, 2)}

    def line(d):
        return {"ctx": lax.rem(group + 2 * d, n_ctx)}

    barrier = pltpu.get_barrier_semaphore()
    for target in (core, far, near):
        pl.semaphore_signal(barrier, inc=1, device_id=target, device_id_type=MESH)

    @pl.loop(1, outer)
    def _(d):
        pl.semaphore_signal(barrier, inc=1, device_id=line(d), device_id_type=MESH)

    pl.semaphore_wait(barrier, outer + 2)

    def copy(src, dst, sem, target):
        return pltpu.make_async_remote_copy(
            src_ref=src, dst_ref=dst, send_sem=send_sem.at[sem], recv_sem=recv_sem.at[sem],
            device_id=target, device_id_type=MESH,
        )

    def cut(k):
        return pl.ds(k * piece, piece)

    def to_core(k):
        return copy(cand_ref.at[1 - side, cut(k)], from_core.at[cut(k)], k, core)

    def to_far(k):
        return copy(merged.at[cut(k)], from_far.at[cut(k)], PIECES + k, far)

    def to_near(k):
        return copy(keys.at[0, side, cut(k)], keys.at[1, side, cut(k)], 2 * PIECES + k, near)

    def share(where, slot, k):
        ref = keys.at[where, slot, cut(k)]
        return copy(ref, ref, (3 + where) * PIECES + k, core)

    first = 5 * PIECES
    base_copy = copy(base_ref, base_near, first, near)

    def query_copy(d):
        return copy(own_q_ref, heads.at[d], first + d, line(d))

    def part_copy(d):
        return copy(part_send.at[d], part_recv.at[d], first + outer + d, line(outer - d))

    def stat_copy(d):
        return copy(stat_send.at[d], stat_recv.at[d], first + 2 * outer + d, line(outer - d))

    for k in range(PIECES):
        to_core(k).start()
    base_copy.start()

    @pl.loop(1, outer)
    def _(d):
        query_copy(d).start()

    for k in range(PIECES):
        to_core(k).wait_recv()
        merged[cut(k), :] = cand_ref[side, cut(k), :] + from_core[cut(k), :]
        to_far(k).start()

    limits = limit_ref[...]

    def begin():
        acc[...] = jnp.zeros_like(acc)
        peak_ref[...] = jnp.full_like(peak_ref, -1e30)
        total_ref[...] = jnp.zeros_like(total_ref)

    def absorb(query_rows, where, slot, start, base):
        key_rows = keys[where, slot, pl.ds(start, SPAN), :]
        score = lax.dot_general(
            query_rows, key_rows, (((1,), (1,)), ((), ())), preferred_element_type=jnp.float32
        ) * (QK ** (-0.5))
        position = base + start + lax.broadcasted_iota(jnp.int32, (1, SPAN), 1)
        visible = position < limits[:, :1]
        old = peak_ref[...]
        new = jnp.maximum(old, jnp.max(jnp.where(visible, score, -1e30), axis=1, keepdims=True))
        weight = jnp.exp(jnp.where(visible, score - new[:, :1], -1e30)).astype(jnp.bfloat16)
        shrink = jnp.exp(old - new)
        peak_ref[...] = new
        total_ref[...] = total_ref[...] * shrink + jnp.sum(
            weight.astype(jnp.float32), axis=1, keepdims=True
        )
        acc[...] = acc[...] * shrink[:, :1] + jnp.dot(
            weight, key_rows[:, :LAT], preferred_element_type=jnp.float32
        )

    def base_of(where, slot):
        ref = base_ref if where == 0 else base_near
        row = ref[slot : slot + 1, :]
        return jnp.concatenate([row] * (SPAN // LANES), axis=1)

    def finish():
        total = total_ref[...]
        lane = lax.broadcasted_iota(jnp.int32, (rows, LANES), 1)
        stats = jnp.where(lane < 4, peak_ref[...], total)
        if rows % LANES:
            stats = jnp.concatenate(
                [stats, jnp.zeros((LANES - rows % LANES, LANES), jnp.float32)], axis=0
            )
        inverse = 1.0 / jnp.maximum(total, 1e-30)
        return acc[...] * inverse[:, :1], jnp.transpose(stats)[:8, :]

    begin()
    own_rows = own_q_ref[...]
    base_copy.wait_recv()

    def pass_on(k):
        to_near(k).wait_recv()
        share(1, side, k).start()

    per_span = SPAN // piece
    for k in range(PIECES):
        to_far(k).wait_recv()
        keys[0, side, cut(k), :] = merged[cut(k), :] + from_far[cut(k), :]
        to_near(k).start()
        share(0, side, k).start()
        if k >= 2:
            pass_on(k - 2)
        share(0, 1 - side, k).wait_recv()
        if k % per_span == per_span - 1:
            start = (k // per_span) * SPAN
            for slot in range(HOT_GRP):
                absorb(own_rows, 0, slot, start, base_of(0, slot))
    for k in range(max(PIECES - 2, 0), PIECES):
        pass_on(k)
    for k in range(PIECES):
        share(1, 1 - side, k).wait_recv()
        if k % per_span == per_span - 1:
            start = (k // per_span) * SPAN
            for slot in range(HOT_GRP):
                absorb(own_rows, 1, slot, start, base_of(1, slot))
    part, stats = finish()
    part_own[...] = part
    stat_recv[0] = stats

    @pl.loop(1, outer)
    def _(d):
        query_copy(d).wait_recv()
        begin()
        query_rows = heads[d]
        for where in range(2):
            for slot in range(HOT_GRP):
                base = base_of(where, slot)
                for start in range(0, BLK, SPAN):
                    absorb(query_rows, where, slot, start, base)
        part, stats = finish()
        stat_send[d] = stats
        part_send[d] = part.astype(jnp.bfloat16)
        stat_copy(d).start()
        part_copy(d).start()

    for k in range(PIECES):
        to_core(k).wait_send()
        to_far(k).wait_send()
        to_near(k).wait_send()
        share(0, side, k).wait_send()
        share(1, side, k).wait_send()
    base_copy.wait_send()

    @pl.loop(1, outer)
    def _(d):
        query_copy(d).wait_send()
        stat_copy(d).wait()

    every = [stat_recv[d] for d in range(outer)]
    overall = functools.reduce(jnp.maximum, [s[:1, :] for s in every])
    shares = [jnp.exp(s[:1, :] - overall) * s[4:5, :] for s in every]
    inverse = 1.0 / functools.reduce(jnp.add, shares)

    def column(d):
        across = jnp.broadcast_to(shares[d] * inverse, (LANES, shares[d].shape[1]))
        return jnp.transpose(across)[:rows, :1]

    acc[...] = part_own[...] * column(0)
    for d in range(1, outer):
        part_copy(d).wait()
        acc[...] += part_recv[d].astype(jnp.float32) * column(d)
    out_ref[...] = acc[...].astype(out_ref.dtype)


def on_device(latents, queries, hot_ids, lengths):
    width = LAT + ROPE
    padded = -(-width // LANES) * LANES
    n_rep = lax.axis_size("rep")
    n_ctx = lax.axis_size("ctx")
    group = lax.axis_index("ctx")
    me = lax.axis_index("rep")
    per_device = latents.shape[0] // BLK
    found = []
    for slot in range(HOT_GRP):
        block = lax.dynamic_slice_in_dim(latents, hot_ids[slot] % per_device * BLK, BLK, 0)
        found.append(jnp.where(hot_ids[slot] // per_device == me, block, jnp.zeros_like(block)))
    cand = jnp.pad(jnp.stack(found), ((0, 0), (0, 0), (0, padded - width)))
    count = queries.shape[0]
    local = queries.shape[1] // width
    rows = count * local
    own_q = jnp.pad(queries.reshape(rows, width), ((0, 0), (0, padded - width)))
    base = (group * (n_rep * per_device) + hot_ids) * BLK
    base = jnp.broadcast_to(jnp.pad(base, (0, 8 - HOT_GRP))[:, None], (8, LANES))
    limit = jnp.broadcast_to(lengths[:, None, None], (count, local, LANES)).reshape(rows, LANES)
    outer = n_ctx // 2
    wide = -(-rows // LANES) * LANES
    sems = 5 * PIECES + 3 * outer
    vmem = pl.BlockSpec(memory_space=pltpu.VMEM)
    bf16, f32 = jnp.bfloat16, jnp.float32
    out = pl.pallas_call(
        functools.partial(kernel, n_ctx, n_rep),
        out_shape=jax.ShapeDtypeStruct((rows, LAT), bf16),
        in_specs=[vmem] * 4,
        out_specs=vmem,
        scratch_shapes=[
            pltpu.VMEM((BLK, padded), bf16),
            pltpu.VMEM((BLK, padded), bf16),
            pltpu.VMEM((BLK, padded), bf16),
            pltpu.VMEM((2, HOT_GRP, BLK, padded), bf16),
            pltpu.VMEM((outer, rows, padded), bf16),
            pltpu.VMEM((8, LANES), jnp.int32),
            pltpu.VMEM((outer, 8, wide), f32),
            pltpu.VMEM((outer, 8, wide), f32),
            pltpu.VMEM((outer, rows, LAT), bf16),
            pltpu.VMEM((outer, rows, LAT), bf16),
            pltpu.VMEM((rows, LAT), f32),
            pltpu.VMEM((rows, LAT), f32),
            pltpu.VMEM((rows, LANES), f32),
            pltpu.VMEM((rows, LANES), f32),
            pltpu.SemaphoreType.DMA((sems,)),
            pltpu.SemaphoreType.DMA((sems,)),
        ],
        compiler_params=pltpu.CompilerParams(
            collective_id=0, has_side_effects=True, vmem_limit_bytes=48 * 1024 * 1024
        ),
    )(cand, own_q, base, limit)
    return out.reshape(count, local * LAT)


def solution(mesh):
    placed = (P(("ctx", "rep"), None), P("rep", "ctx"), P("ctx"), P("rep"))
    return jax.shard_map(
        on_device, mesh=mesh, in_specs=placed, out_specs=P("rep", "ctx"), check_vma=False
    )
```

time: 255 us -> 92.2 us (0.36)
  waiting for transfers between devices: 153 us -> 0 us
  Pallas kernels: 0 us -> 77.7 us
  matrix products: 22.7 us -> 0 us
  local copies, waits for them, and re-layouts: 29.3 us -> 8.57 us
  between operations: 20 us -> 5.05 us
  starting transfers between devices: 14.8 us -> 0 us
  other arithmetic: 14 us -> 0.54 us
    all_to_all x3 -> x0, waiting for transfers between devices: 94.8 us -> none  [the longest x1 89.8 us: on_device(): lax.all_to_all(numerators[None], 'ctx', split_axis=2, concat_axis=0, tile...]
    pallas_call x0 -> x1, Pallas kernels: none -> 77.7 us  [on_device(): pl.pallas_call(functools.partial(kernel, n_ctx, n_rep), out_shape=jax.Sha...]
    psum x1 -> x0, waiting for transfers between devices: 57.9 us -> none  [from_root(): return lax.psum(block, axis)]
    dot_general x8 -> x0, matrix products: 22.7 us -> none  [the longest x4 13.4 us: partial_value(): jnp.einsum('qhw,kw->qhk', query_block, key_rows, preferred_element_type=j...]
    all_to_all x3 -> x0, starting transfers between devices: 14.8 us -> none  [the longest x1 5.93 us: on_device(): lax.all_to_all(numerators[None], 'ctx', split_axis=2, concat_axis=0, tile...]
    unnamed x12 -> x8, local copies, waits for them, and re-layouts: 11.9 us -> 2.95 us
    reduce_sum x6 -> x0, other arithmetic: 6.94 us -> none  [the longest x4 4.33 us: partial_value(): totals = jnp.sum(weights, axis=2, dtype=jnp.float32)]
    another operation x3 -> x0, local copies, waits for them, and re-layouts: 6.79 us -> none  [the longest x1 6.59 us: on_device(): numerators[None]]
  transfers between devices with their start and end apart: 5 -> 0, of which waited for: 3 -> 0; matrix products, arithmetic and copies ran while one was open for 7% -> 0% of each run, Pallas kernels for 0% -> 0%
where the time goes in v1:
time: 92.2 us; the launch traced here: 91.9 us
  Pallas kernels  77.7 us (84%)
  local copies, waits for them, and re-layouts  8.57 us (9%)
  between operations  5.05 us (5%)
    pallas_call x1, Pallas kernels, on_device(): pl.pallas_call(functools.partial(kernel, n_ctx, n_rep), out_shape=jax.Sha...  77.7 us
    unnamed x8, local copies, waits for them, and re-layouts  2.95 us
    dynamic_slice x1, local copies, waits for them, and re-layouts, on_device(): lax.dynamic_slice_in_dim(latents, hot_ids[slot] % per_device * BLK, BLK, 0)  2.85 us

profile of v1, /device:TPU:0, one launch (start us, length us, event | category | flops | bytes accessed | tf_op | source)
XLA Modules:
  0.0 91.9 jit_solution(10227638837566527450)
XLA Ops:
  0.0 1.3 %fusion.3 = (s32[1]{0:T(128)}, s32[1]{0:T(128)}) fusion(s32[2]{0:T(128)} %param.6), kind=kLoop, calls=%fused_computation.9 | loop fusion | bytes 16 | tf_op jit(solution)/shard_map/slice | solution.py:228
  5.0 2.9 %constant_dynamic-slice_fusion.1 = (bf16[1024,576]{0,1:T(8,128)(2,1)}, bf16[1024,576]{0,1:T(8,128)(2,1)S(1)}) fusion(bf16[4096,576]{0,1:T(8,128)(2,1)} %param.4, s32[]{:T(128)S(6)} %select_n.41, s32[]{:T(128)S(6)} %select_n.46), kind=kLoop, calls=%fused_computation.8 | loop fusion | bytes 4718600 | tf_op jit(solution)/shard_map/dynamic_slice | solution.py:227
  7.8 0.7 copy.10
  8.6 1.7 %copy.9 = bf16[1024,576]{1,0:T(8,128)(2,1)S(1)} copy(bf16[1024,576]{0,1:T(8,128)(2,1)} %get-tuple-element.5) | data formatting | bytes 2359296
  11.5 0.2 select_bitcast_fusion
  11.7 0.0 copy-start.1
  11.8 0.0 copy-start
  11.8 0.0 copy-start.2
  11.8 0.3 fusion.2.cand_ref
  12.1 0.3 copy-done.1
  12.4 0.1 broadcast_in_dim.16.base_ref
  12.5 0.2 copy-done
  12.7 0.3 reshape.10
  13.1 0.0 copy-done.2
  13.1 0.1 broadcast_in_dim.17
  13.1 0.1 broadcast_in_dim.18
  13.2 0.1 broadcast_in_dim.19.limit_ref
  13.3 77.7 %shard_map.46 = bf16[256,512]{1,0:T(8,128)(2,1)S(1)} custom-call(bf16[2,1024,640]{2,1,0:T(8,128)(2,1)S(1)} %fusion.2.cand_ref, bf16[256,640]{1,0:T(8,128)(2,1)S(1)} %pad.13.own_q_ref, s32[8,128]{1,0:T(8,128)S(1)} %broadcast_in_dim.16.base_ref, s32[256,128]{1,0:T(8,128)S(1)} %broadcast_in_dim.19.limit_ref), custom_call_target="tpu_custom_call" | custom-call | tf_op jit(solution)/shard_map/pallas_call | solution.py:242
  91.1 0.8 reshape.11
  (3 shorter events, 0.0 us)
Async XLA Ops:
  11.7 0.7 copy-start.1
  11.8 1.0 %copy-start = (bf16[16,9216]{1,0:T(8,128)(2,1)S(1)}, bf16[16,9216]{1,0:T(8,128)(2,1)}, u32[]{:S(2)}) copy-start(bf16[16,9216]{1,0:T(8,128)(2,1)} %param.5) | copy-start | bytes 884740
  11.8 1.3 %copy-start.2 = (s32[16]{0:T(128)S(1)}, s32[16]{0:T(128)}, u32[]{:S(2)}) copy-start(s32[16]{0:T(128)} %param.7) | copy-start | bytes 196

commit v2 on v1

v2 whole, which is shorter than its diff:
```python
import functools

import jax
import jax.numpy as jnp
from jax import lax
from jax.experimental import pallas as pl
from jax.experimental.pallas import tpu as pltpu
from jax.sharding import PartitionSpec as P

H = 128
LAT = 512
ROPE = 64
QK = 192
BLK = 1024
HOT_GRP = 2
LANES = 128
PIECES = 8
SPAN = 512
MESH = pl.DeviceIdType.MESH


def kernel(
    n_ctx, n_rep, latent_ref, query_ref, hot_ref, length_ref, out_ref,
    cand, from_core, merged, from_far, keys, heads, base_own, base_near, stat_send, stat_recv,
    part_send, part_recv, acc, peaks, totals, send_sem, recv_sem,
):
    outer = n_ctx // 2
    count = query_ref.shape[0]
    width = latent_ref.shape[0]
    local = query_ref.shape[1] // width
    rows = count * local
    per_device = latent_ref.shape[1] // BLK
    piece = BLK // PIECES
    group = lax.axis_index("ctx")
    rep = lax.axis_index("rep")
    side = lax.rem(rep, 2)
    core = {"rep": rep + 1 - 2 * side}
    far = {"rep": lax.rem(rep + n_rep // 2, n_rep)}
    near = {"ctx": group + 1 - 2 * lax.rem(group, 2)}

    def line(d):
        return {"ctx": lax.rem(group + 2 * d, n_ctx)}

    barrier = pltpu.get_barrier_semaphore()
    for target in (core, far, near):
        pl.semaphore_signal(barrier, inc=1, device_id=target, device_id_type=MESH)

    @pl.loop(1, outer)
    def _(d):
        pl.semaphore_signal(barrier, inc=1, device_id=line(d), device_id_type=MESH)

    def factors(slot):
        hot = jnp.full((1, LANES), hot_ref[slot], jnp.int32)
        return [
            jnp.where(hot == rep * per_device + b, 1.0, 0.0).astype(jnp.bfloat16)
            for b in range(per_device)
        ]

    other_factors = factors(1 - side)
    own_factors = factors(side)

    def held(chosen, k):
        return functools.reduce(
            jnp.add,
            [
                latent_ref[:, b * BLK + k * piece : b * BLK + (k + 1) * piece] * chosen[b]
                for b in range(per_device)
            ],
        )

    cand[0] = held(other_factors, 0)
    pl.semaphore_wait(barrier, outer + 2)

    def copy(src, dst, sem, target):
        return pltpu.make_async_remote_copy(
            src_ref=src, dst_ref=dst, send_sem=send_sem.at[sem], recv_sem=recv_sem.at[sem],
            device_id=target, device_id_type=MESH,
        )

    def to_core(k):
        return copy(cand.at[k], from_core.at[k], k, core)

    def to_far(k):
        return copy(merged.at[k], from_far.at[k], PIECES + k, far)

    def to_near(k):
        return copy(keys.at[0, side, k], keys.at[1, side, k], 2 * PIECES + k, near)

    def share(where, slot, k):
        ref = keys.at[where, slot, k]
        return copy(ref, ref, (3 + where) * PIECES + k, core)

    first = 5 * PIECES
    base_copy = copy(base_own, base_near, first, near)

    def query_copy(d):
        return copy(heads.at[0], heads.at[d], first + d, line(d))

    def part_copy(d):
        return copy(part_send.at[d], part_recv.at[d], first + outer + d, line(outer - d))

    def stat_copy(d):
        return copy(stat_send.at[d], stat_recv.at[d], first + 2 * outer + d, line(outer - d))

    to_core(0).start()
    for k in range(1, PIECES):
        cand[k] = held(other_factors, k)
        to_core(k).start()
    for h in range(local):
        heads[0, h * count : (h + 1) * count, :] = query_ref[:, h * width : (h + 1) * width]
    slot_row = lax.broadcasted_iota(jnp.int32, (8, LANES), 0)
    base = jnp.zeros((8, LANES), jnp.int32)
    for slot in range(HOT_GRP):
        at = (group * (n_rep * per_device) + hot_ref[slot]) * BLK
        base = jnp.where(slot_row == slot, at, base)
    base_own[...] = base

    for k in range(PIECES):
        to_core(k).wait_recv()
        merged[k] = held(own_factors, k) + from_core[k]
        to_far(k).start()
        if k == 0:
            @pl.loop(1, outer)
            def _(d):
                query_copy(d).start()
            base_copy.start()

    query_row = lax.broadcasted_iota(jnp.int32, (count, LANES), 0)
    limit = jnp.zeros((count, LANES), jnp.int32)
    for q in range(count):
        limit = jnp.where(query_row == q, length_ref[q], limit)
    limits = jnp.concatenate([limit] * local, axis=0)[:, :1]

    acc[...] = jnp.zeros_like(acc)
    peaks[...] = jnp.full_like(peaks, -1e30)
    totals[...] = jnp.zeros_like(totals)
    per_span = SPAN // piece

    def absorb(d, where, slot, span):
        key_cols = jnp.concatenate(
            [keys[where, slot, span * per_span + i] for i in range(per_span)], axis=1
        )
        score = jnp.dot(
            heads[d], key_cols, preferred_element_type=jnp.float32
        ) * (QK ** (-0.5))
        ref = base_own if where == 0 else base_near
        base = jnp.concatenate([ref[slot : slot + 1, :]] * (SPAN // LANES), axis=1)
        position = base + span * SPAN + lax.broadcasted_iota(jnp.int32, (1, SPAN), 1)
        visible = position < limits
        score = jnp.where(visible, score, -1e30)
        old = peaks[d]
        new = jnp.maximum(old, jnp.max(score, axis=1, keepdims=True))
        weight = jnp.exp(jnp.where(visible, score - new[:, :1], -1e30)).astype(jnp.bfloat16)
        shrink = jnp.exp(old - new)
        peaks[d] = new
        totals[d] = totals[d] * shrink + jnp.sum(
            weight.astype(jnp.float32), axis=1, keepdims=True
        )
        acc[d] = acc[d] * shrink[:, :1] + lax.dot_general(
            weight, key_cols[:LAT, :], (((1,), (1,)), ((), ())),
            preferred_element_type=jnp.float32,
        )

    def absorb_rest(where, slot, span):
        @pl.loop(1, outer)
        def _(d):
            absorb(d, where, slot, span)

    def finish(d):
        total = totals[d]
        lane = lax.broadcasted_iota(jnp.int32, (rows, LANES), 1)
        stats = jnp.where(lane < 4, peaks[d], total)
        if rows % LANES:
            stats = jnp.concatenate(
                [stats, jnp.zeros((LANES - rows % LANES, LANES), jnp.float32)], axis=0
            )
        inverse = 1.0 / jnp.maximum(total, 1e-30)
        return acc[d] * inverse[:, :1], jnp.transpose(stats)[:8, :]

    def pass_on(k):
        to_near(k).wait_recv()
        share(1, side, k).start()
        share(1, 1 - side, k).wait_recv()

    spans = BLK // SPAN
    waiting = []
    base_copy.wait_recv()
    for k in range(PIECES + 2):
        if k < PIECES:
            to_far(k).wait_recv()
            keys[0, side, k] = merged[k] + from_far[k]
            to_near(k).start()
            share(0, side, k).start()
            share(0, 1 - side, k).wait_recv()
            if k % per_span == per_span - 1:
                for slot in range(HOT_GRP):
                    absorb(0, 0, slot, k // per_span)
                    waiting.append((0, slot, k // per_span))
        if k >= 2:
            pass_on(k - 2)
            if (k - 2) % per_span == per_span - 1 and (k - 2) // per_span < spans - 1:
                for slot in range(HOT_GRP):
                    absorb(0, 1, slot, (k - 2) // per_span)
                    waiting.append((1, slot, (k - 2) // per_span))
        if k == PIECES - 2:
            @pl.loop(1, outer)
            def _(d):
                query_copy(d).wait_recv()
        if k >= PIECES - 2:
            for task in waiting[:2]:
                absorb_rest(*task)
            waiting = waiting[2:]
    for task in waiting:
        absorb_rest(*task)

    @pl.loop(1, outer)
    def _(d):
        for slot in range(HOT_GRP):
            absorb(d, 1, slot, spans - 1)
        part, stats = finish(d)
        stat_send[d] = stats
        part_send[d] = part.astype(jnp.bfloat16)
        stat_copy(d).start()
        part_copy(d).start()

    for slot in range(HOT_GRP):
        absorb(0, 1, slot, spans - 1)
    part, stats = finish(0)
    acc[0] = part
    stat_recv[0] = stats

    for k in range(PIECES):
        to_core(k).wait_send()
        to_far(k).wait_send()
        to_near(k).wait_send()
        share(0, side, k).wait_send()
        share(1, side, k).wait_send()
    base_copy.wait_send()

    @pl.loop(1, outer)
    def _(d):
        query_copy(d).wait_send()
        stat_copy(d).wait()

    every = [stat_recv[d] for d in range(outer)]
    overall = functools.reduce(jnp.maximum, [s[:1, :] for s in every])
    shares = [jnp.exp(s[:1, :] - overall) * s[4:5, :] for s in every]
    inverse = 1.0 / functools.reduce(jnp.add, shares)

    def column(d):
        across = jnp.broadcast_to(shares[d] * inverse, (LANES, shares[d].shape[1]))
        return jnp.transpose(across)[:rows, :1]

    acc[0] = acc[0] * column(0)
    for d in range(1, outer):
        part_copy(d).wait()
        acc[0] += part_recv[d].astype(jnp.float32) * column(d)
    for h in range(local):
        out_ref[:, h * LAT : (h + 1) * LAT] = acc[0, h * count : (h + 1) * count, :].astype(
            out_ref.dtype
        )


def on_device(latents, queries, hot_ids, lengths):
    width = LAT + ROPE
    n_rep = lax.axis_size("rep")
    n_ctx = lax.axis_size("ctx")
    count = queries.shape[0]
    local = queries.shape[1] // width
    rows = count * local
    outer = n_ctx // 2
    wide = -(-rows // LANES) * LANES
    piece = BLK // PIECES
    sems = 5 * PIECES + 3 * outer
    vmem = pl.BlockSpec(memory_space=pltpu.VMEM)
    smem = pl.BlockSpec(memory_space=pltpu.SMEM)
    bf16, f32 = jnp.bfloat16, jnp.float32
    return pl.pallas_call(
        functools.partial(kernel, n_ctx, n_rep),
        out_shape=jax.ShapeDtypeStruct((count, local * LAT), bf16),
        in_specs=[vmem, vmem, smem, smem],
        out_specs=vmem,
        scratch_shapes=[
            pltpu.VMEM((PIECES, width, piece), bf16),
            pltpu.VMEM((PIECES, width, piece), bf16),
            pltpu.VMEM((PIECES, width, piece), bf16),
            pltpu.VMEM((PIECES, width, piece), bf16),
            pltpu.VMEM((2, HOT_GRP, PIECES, width, piece), bf16),
            pltpu.VMEM((outer, rows, width), bf16),
            pltpu.VMEM((8, LANES), jnp.int32),
            pltpu.VMEM((8, LANES), jnp.int32),
            pltpu.VMEM((outer, 8, wide), f32),
            pltpu.VMEM((outer, 8, wide), f32),
            pltpu.VMEM((outer, rows, LAT), bf16),
            pltpu.VMEM((outer, rows, LAT), bf16),
            pltpu.VMEM((outer, rows, LAT), f32),
            pltpu.VMEM((outer, rows, LANES), f32),
            pltpu.VMEM((outer, rows, LANES), f32),
            pltpu.SemaphoreType.DMA((sems,)),
            pltpu.SemaphoreType.DMA((sems,)),
        ],
        compiler_params=pltpu.CompilerParams(
            collective_id=0, has_side_effects=True, vmem_limit_bytes=56 * 1024 * 1024
        ),
    )(latents.T, queries, hot_ids, lengths)


def solution(mesh):
    placed = (P(("ctx", "rep"), None), P("rep", "ctx"), P("ctx"), P("rep"))
    return jax.shard_map(
        on_device, mesh=mesh, in_specs=placed, out_specs=P("rep", "ctx"), check_vma=False
    )
```

time: 92.2 us -> 87.4 us (0.948)
  Pallas kernels: 77.7 us -> 85.6 us
  local copies, waits for them, and re-layouts: 8.57 us -> 1.67 us
  between operations: 5.05 us -> 0.01 us
    pallas_call x1, Pallas kernels: 77.7 us -> 85.6 us  [on_device(): pl.pallas_call(functools.partial(kernel, n_ctx, n_rep), out_shape=jax.Sha...]
    dynamic_slice x1 -> x0, local copies, waits for them, and re-layouts: 2.85 us -> none  [on_device(): lax.dynamic_slice_in_dim(latents, hot_ids[slot] % per_device * BLK, BLK, 0)]
    slice x1 -> x0, local copies, waits for them, and re-layouts: 1.3 us -> none  [on_device(): hot_ids[slot] // per_device == me]
    unnamed x8 -> x1, local copies, waits for them, and re-layouts: 2.95 us -> 1.67 us
    reshape x2 -> x0, local copies, waits for them, and re-layouts: 1.11 us -> none  [the longest x1 0.83 us: on_device(): return out.reshape(count, local * LAT)]
where the time goes in v2:
time: 87.4 us; the launch traced here: 87.3 us
  Pallas kernels  85.6 us (98%)
  local copies, waits for them, and re-layouts  1.67 us (2%)
    pallas_call x1, Pallas kernels, on_device(): pl.pallas_call(functools.partial(kernel, n_ctx, n_rep), out_shape=jax.Sha...  85.6 us

profile of v2, /device:TPU:0, one launch (start us, length us, event | category | flops | bytes accessed | tf_op | source)
XLA Modules:
  0.0 87.3 jit_solution(13106458616672869469)
XLA Ops:
  0.0 85.6 %shard_map.46 = bf16[16,8192]{1,0:T(8,128)(2,1)} custom-call(bf16[576,4096]{1,0:T(8,128)(2,1)} %bitcast.1, bf16[16,9216]{1,0:T(8,128)(2,1)} %query_ref.1, s32[2]{0:T(128)} %hot_ref.1, s32[16]{0:T(128)} %length_ref.1), custom_call_target="tpu_custom_call" | custom-call | tf_op jit(solution)/shard_map/pallas_call | solution.py:278
  85.6 1.7 %copy.6 = bf16[16,8192]{1,0:T(8,128)(2,1)} copy(bf16[16,8192]{1,0:T(8,128)(2,1)} %shard_map.46) | data formatting | bytes 524288

commit v3 on v2

--- a/solution.py
+++ b/solution.py
@@ -15,7 +15,7 @@
 HOT_GRP = 2
 LANES = 128
 PIECES = 8
-SPAN = 512
+SPAN = 1024
 MESH = pl.DeviceIdType.MESH
 
 
@@ -180,43 +180,38 @@
     def pass_on(k):
         to_near(k).wait_recv()
         share(1, side, k).start()
-        share(1, 1 - side, k).wait_recv()
-
-    spans = BLK // SPAN
-    waiting = []
+
     base_copy.wait_recv()
-    for k in range(PIECES + 2):
-        if k < PIECES:
-            to_far(k).wait_recv()
-            keys[0, side, k] = merged[k] + from_far[k]
-            to_near(k).start()
-            share(0, side, k).start()
-            share(0, 1 - side, k).wait_recv()
-            if k % per_span == per_span - 1:
-                for slot in range(HOT_GRP):
-                    absorb(0, 0, slot, k // per_span)
-                    waiting.append((0, slot, k // per_span))
+    for k in range(PIECES):
+        to_far(k).wait_recv()
+        keys[0, side, k] = merged[k] + from_far[k]
+        to_near(k).start()
+        share(0, side, k).start()
         if k >= 2:
             pass_on(k - 2)
-            if (k - 2) % per_span == per_span - 1 and (k - 2) // per_span < spans - 1:
-                for slot in range(HOT_GRP):
-                    absorb(0, 1, slot, (k - 2) // per_span)
-                    waiting.append((1, slot, (k - 2) // per_span))
-        if k == PIECES - 2:
-            @pl.loop(1, outer)
-            def _(d):
-                query_copy(d).wait_recv()
-        if k >= PIECES - 2:
-            for task in waiting[:2]:
-                absorb_rest(*task)
-            waiting = waiting[2:]
-    for task in waiting:
-        absorb_rest(*task)
+    for k in range(PIECES):
+        share(0, 1 - side, k).wait_recv()
+    spans = BLK // SPAN
+    for slot in range(HOT_GRP):
+        for span in range(spans):
+            absorb(0, 0, slot, span)
+
+    @pl.loop(1, outer)
+    def _(d):
+        query_copy(d).wait_recv()
+
+    for slot in range(HOT_GRP):
+        pass_on(PIECES - HOT_GRP + slot)
+        for span in range(spans):
+            absorb_rest(0, slot, span)
+    for k in range(PIECES):
+        share(1, 1 - side, k).wait_recv()
 
     @pl.loop(1, outer)
     def _(d):
         for slot in range(HOT_GRP):
-            absorb(d, 1, slot, spans - 1)
+            for span in range(spans):
+                absorb(d, 1, slot, span)
         part, stats = finish(d)
         stat_send[d] = stats
         part_send[d] = part.astype(jnp.bfloat16)
@@ -224,7 +219,8 @@
         part_copy(d).start()
 
     for slot in range(HOT_GRP):
-        absorb(0, 1, slot, spans - 1)
+        for span in range(spans):
+            absorb(0, 1, slot, span)
     part, stats = finish(0)
     acc[0] = part
     stat_recv[0] = stats

time: 87.4 us -> 78.7 us (0.900)
  Pallas kernels: 85.6 us -> 76.9 us
    pallas_call x1, Pallas kernels: 85.6 us -> 76.9 us  [on_device(): pl.pallas_call(functools.partial(kernel, n_ctx, n_rep), out_shape=jax.Sha...]
where the time goes in v3:
time: 78.7 us; the launch traced here: 78.6 us
  Pallas kernels  76.9 us (98%)
  local copies, waits for them, and re-layouts  1.67 us (2%)
    pallas_call x1, Pallas kernels, on_device(): pl.pallas_call(functools.partial(kernel, n_ctx, n_rep), out_shape=jax.Sha...  76.9 us
    unnamed x1, local copies, waits for them, and re-layouts  1.67 us

profile of v3, /device:TPU:0, one launch (start us, length us, event | category | flops | bytes accessed | tf_op | source)
XLA Modules:
  0.0 78.6 jit_solution(15634693655920393639)
XLA Ops:
  0.0 76.9 %shard_map.46 = bf16[16,8192]{1,0:T(8,128)(2,1)} custom-call(bf16[576,4096]{1,0:T(8,128)(2,1)} %bitcast.1, bf16[16,9216]{1,0:T(8,128)(2,1)} %query_ref.1, s32[2]{0:T(128)} %hot_ref.1, s32[16]{0:T(128)} %length_ref.1), custom_call_target="tpu_custom_call" | custom-call | tf_op jit(solution)/shard_map/pallas_call | solution.py:274
  76.9 1.7 %copy.6 = bf16[16,8192]{1,0:T(8,128)(2,1)} copy(bf16[16,8192]{1,0:T(8,128)(2,1)} %shard_map.46) | data formatting | bytes 524288
